TPU v7x, 16 devices: a whole 2x2x2 slice. The times are simulated.
16 devices in a mesh: data: 16 (over z, y, x, core).
Axes of the slice: x: 2, y: 2, z: 2, core: 2. Of those that a mesh axis runs over, the one named last changes fastest.
Arguments:
- x_in: bfloat16 [32768, 768], P('data')
- dy_in: bfloat16 [32768, 768], P('data')
- weights: bfloat16 [4, 768, 768], replicated
- a_old: float32 [3072, 768], P('data')
- s_old: float32 [3072, 768], P('data')
- a_inv: float32 [3072, 768], P('data')
- s_inv: float32 [4, 768, 768], replicated
Outputs:
- output 1: float32 [4, 768, 768], replicated
- output 2: float32 [3072, 768], P('data')
- output 3: float32 [3072, 768], P('data')
All inputs are finite; a program needn't handle non-finite values.
Results may differ from a plain program's by a relative error of at most 0.00184902.
Values are sent between devices in bfloat16 or wider.
A program may use at most 1 GiB of HBM per device.

v0:
```python
import functools
import jax
import jax.numpy as jnp
from jax import lax
from jax.sharding import PartitionSpec as P

FACTOR_DECAY = 0.75
PRECISE = lax.Precision.HIGHEST


def gelu_grad(pre_act, d_act):
    pullback = jax.vjp(functools.partial(jax.nn.gelu, approximate=True), pre_act.astype(jnp.float32))[1]
    return pullback(d_act.astype(jnp.float32))[0].astype(jnp.bfloat16)


def cross_rows(left_op, right_op):
    return jnp.einsum("bi,bj->ij", left_op, right_op, preferred_element_type=jnp.float32)


def local_pass(x_loc, dy_loc, weights):
    n_layers = weights.shape[0]
    layer_inputs = [x_loc]
    pre_acts = []
    for layer_id in range(n_layers - 1):
        pre_act = jnp.dot(layer_inputs[layer_id], weights[layer_id], preferred_element_type=jnp.float32).astype(jnp.bfloat16)
        pre_acts.append(pre_act)
        layer_inputs.append(jax.nn.gelu(pre_act.astype(jnp.float32), approximate=True).astype(jnp.bfloat16))
    out_grads = [dy_loc] * n_layers
    for layer_id in range(n_layers - 1, 0, -1):
        d_act = jnp.einsum("bj,ij->bi", out_grads[layer_id], weights[layer_id], preferred_element_type=jnp.float32).astype(jnp.bfloat16)
        out_grads[layer_id - 1] = gelu_grad(pre_acts[layer_id - 1], d_act)
    return layer_inputs, out_grads


def solution(mesh):
    n_dev = mesh.shape["data"]

    def device_step(x_loc, dy_loc, weights, a_old_rows, s_old_rows, a_inv_rows, s_inv):
        n_layers = weights.shape[0]
        model_width = weights.shape[1]
        batch_total = x_loc.shape[0] * n_dev
        layer_inputs, out_grads = local_pass(x_loc, dy_loc, weights)
        a_loc = jnp.concatenate([cross_rows(h_in, h_in) for h_in in layer_inputs], axis=0) / batch_total
        s_loc = jnp.concatenate([cross_rows(g_out, g_out) for g_out in out_grads], axis=0) / batch_total
        w_loc = jnp.stack([cross_rows(h_in, g_out) for h_in, g_out in zip(layer_inputs, out_grads)]) / batch_total
        a_sum = lax.psum_scatter(a_loc, "data", scatter_dimension=0, tiled=True)
        s_sum = lax.psum_scatter(s_loc, "data", scatter_dimension=0, tiled=True)
        w_grad = lax.psum(w_loc, "data")
        own_rows = a_old_rows.shape[0]
        layer_id = (lax.axis_index("data") * own_rows) // model_width
        w_grad_own = lax.dynamic_index_in_dim(w_grad, layer_id, axis=0, keepdims=False)
        s_inv_own = lax.dynamic_index_in_dim(s_inv, layer_id, axis=0, keepdims=False)
        left_prod = jnp.dot(a_inv_rows, w_grad_own, precision=PRECISE)
        u_rows = jnp.dot(left_prod, s_inv_own, precision=PRECISE)
        u_full = lax.all_gather(u_rows, "data", axis=0, tiled=True).reshape(n_layers, model_width, model_width)
        a_new = FACTOR_DECAY * a_old_rows + (1.0 - FACTOR_DECAY) * a_sum
        s_new = FACTOR_DECAY * s_old_rows + (1.0 - FACTOR_DECAY) * s_sum
        return u_full, a_new, s_new

    row_spec = P("data", None)
    return jax.shard_map(
        device_step,
        mesh=mesh,
        in_specs=(row_spec, row_spec, P(), row_spec, row_spec, row_spec, P()),
        out_specs=(P(), row_spec, row_spec),
        check_vma=False,
    )
```

profile of v0, /device:TPU:0, one launch (start us, length us, event | category | flops | bytes accessed | tf_op | source)
XLA Modules:
  0.0 418.5 jit_solution(1386467419137810113)
XLA Ops:
  7.2 0.0 copy-start
  7.2 0.0 all-reduce.2.cloned.1.call-start
  7.2 1.8 copy-done
  9.1 4.2 %convolution_convert_fusion.4 = bf16[2048,768]{1,0:T(8,128)(2,1)S(1)} fusion(bf16[2048,768]{1,0:T(8,128)(2,1)S(1)} %copy-done, bf16[4,768,768]{2,1,0:T(8,128)(2,1)} %param.9), kind=kOutput, calls=%fused_computation.58 | convolution fusion | flops 2417491968 | bytes 7471104 | tf_op jit(solution)/shard_map/dot_general | solution.py:25
  13.3 0.0 copy-done.1
  13.3 0.0 copy-start.9
  13.3 4.2 %convolution_convert_fusion.3 = bf16[2048,768]{1,0:T(8,128)(2,1)S(1)} fusion(bf16[4,768,768]{2,1,0:T(8,128)(2,1)S(1)} %copy-done.1, bf16[2048,768]{1,0:T(8,128)(2,1)S(1)} %convolution_convert_fusion.4), kind=kOutput, calls=%fused_computation.57 | convolution fusion | flops 2433220608 | bytes 7471104 | tf_op jit(solution)/shard_map/dot_general | solution.py:25
  17.5 0.0 copy-start.2
  17.5 4.2 convolution_convert_fusion.2
  21.7 3.4 convolution_bitcast_fusion
  25.1 6.2 %fusion.5 = bf16[2048,768]{1,0:T(8,128)(2,1)S(1)} fusion(bf16[2048,768]{1,0:T(8,128)(2,1)S(1)} %convolution_convert_fusion.2, bf16[2048,768]{1,0:T(8,128)(2,1)S(1)} %copy-done.2, bf16[4,768,768]{2,1,0:T(8,128)(2,1)S(1)} %copy-done.1), kind=kOutput, calls=%fused_computation.26 | convolution fusion | flops 2452094976 | bytes 10616832 | tf_op jit(solution)/shard_map/bj,ij->bi/dot_general | solution.py:30
  31.4 3.4 convolution_bitcast_fusion.1
  34.8 6.0 %fusion.8 = bf16[2048,768]{1,0:T(8,128)(2,1)S(1)} fusion(bf16[2048,768]{1,0:T(8,128)(2,1)S(1)} %convolution_convert_fusion.3, bf16[2048,768]{1,0:T(8,128)(2,1)S(1)} %fusion.5, bf16[4,768,768]{2,1,0:T(8,128)(2,1)S(1)} %copy-done.1), kind=kOutput, calls=%fused_computation.29 | convolution fusion | flops 2452094976 | bytes 10616832 | tf_op jit(solution)/shard_map/bj,ij->bi/dot_general | solution.py:30
  40.8 3.3 convolution_bitcast_fusion.2
  44.1 6.0 %fusion.11 = bf16[2048,768]{1,0:T(8,128)(2,1)S(1)} fusion(bf16[2048,768]{1,0:T(8,128)(2,1)S(1)} %convolution_convert_fusion.4, bf16[2048,768]{1,0:T(8,128)(2,1)S(1)} %fusion.8, bf16[4,768,768]{2,1,0:T(8,128)(2,1)S(1)} %copy-done.1), kind=kOutput, calls=%fused_computation.32 | convolution fusion | flops 2452094976 | bytes 10616832 | tf_op jit(solution)/shard_map/bj,ij->bi/dot_general | solution.py:30
  50.1 2.7 convolution_bitcast_fusion.3
  52.8 4.2 %maximum_multiply_fusion = f32[4,768,768]{1,2,0:T(8,128)} fusion(f32[1,768,768]{1,2,0:T(8,128)S(1)} %convolution_bitcast_fusion, f32[1,768,768]{1,2,0:T(8,128)S(1)} %convolution_bitcast_fusion.1, f32[1,768,768]{1,2,0:T(8,128)S(1)} %convolution_bitcast_fusion.2, f32[1,768,768]{1,2,0:T(8,128)S(1)} %convolution_bitcast_fusion.3), kind=kLoop, calls=%fused_computation.15 | loop fusion | flops 9437184 | bytes 18874368 | tf_op jit(solution)/shard_map/div | solution.py:45
  57.0 0.0 all-reduce.2.cloned.1.call-update
  57.0 8.8 %reduce-scatter.3.cloned.1.call-start = ((), (), s32[]{:S(2)}) async-start(), calls=%async_computation.4 | async-start | bytes 10027008 | tf_op jit(solution)/shard_map/reduce_scatter | solution.py:46
  65.9 2.7 fusion.64
  68.6 0.0 copy-done.10
  68.6 0.0 copy-start.14
  68.6 5.0 %fusion.60 = f32[768,768]{1,0:T(8,128)S(1)} fusion(bf16[2048,768]{1,0:T(8,128)(2,1)S(1)} %copy-done.10), kind=kOutput, calls=%fused_computation.88 | convolution fusion | flops 2431647744 | bytes 5505024 | tf_op jit(solution)/shard_map/bi,bj->ij/dot_general | solution.py:17
  73.6 0.0 copy-done.14
  73.6 0.0 copy-start.12
  73.6 5.0 %fusion.56 = f32[768,768]{1,0:T(8,128)S(1)} fusion(bf16[2048,768]{1,0:T(8,128)(2,1)S(1)} %copy-done.14), kind=kOutput, calls=%fused_computation.87 | convolution fusion | flops 2431647744 | bytes 5505024 | tf_op jit(solution)/shard_map/bi,bj->ij/dot_general | solution.py:17
  78.6 5.2 %fusion.53 = f32[768,768]{1,0:T(8,128)S(1)} fusion(bf16[2048,768]{1,0:T(8,128)(2,1)S(1)} %copy-done.12), kind=kOutput, calls=%fused_computation.86 | convolution fusion | flops 2431647744 | bytes 5505024 | tf_op jit(solution)/shard_map/bi,bj->ij/dot_general | solution.py:17
  83.8 4.0 maximum_multiply_fusion.1
  87.7 0.0 reduce-scatter.3.cloned.1.call-update
  87.8 0.0 reduce-scatter.5.cloned.1.call-start
  87.8 5.7 %fusion.68 = f32[768,768]{1,0:T(8,128)S(1)} fusion(bf16[2048,768]{1,0:T(8,128)(2,1)} %param.8), kind=kOutput, calls=%fused_computation.93 | convolution fusion | flops 2415919104 | bytes 5505024 | tf_op jit(solution)/shard_map/bi,bj->ij/dot_general | solution.py:17
  93.5 2.8 fusion.67
  96.3 2.8 fusion.66
  99.1 0.0 copy-done.8
  99.1 2.8 fusion.65
  101.9 4.0 maximum_multiply_fusion.2
  105.8 0.0 reduce-scatter.5.cloned.1.call-update
  105.9 0.3 all-gather.2.cloned.1.call-start
  106.2 74.3 %all-reduce.2.cloned.1.call-done = f32[4,768,768]{1,2,0:T(8,128)} async-done(((f32[4,768,768]{1,2,0:T(8,128)}), f32[4,768,768]{1,2,0:T(8,128)}) %all-reduce.2.cloned.1.call-update) | async-done | bytes 9437200 | tf_op jit(solution)/shard_map/psum | solution.py:48
  180.5 3.8 fusion.35
  184.3 4.4 %fusion.33 = f32[192,768]{1,0:T(8,128)} fusion(f32[768,192]{1,0:T(8,128)S(1)} %fusion.35, f32[4,768,768]{2,1,0:T(8,128)} %param.13, s32[]{:T(128)S(6)} %select_n.11), kind=kOutput, calls=%fused_computation.60 | convolution fusion | flops 1358954496 | bytes 3538948 | tf_op jit(solution)/shard_map/dot_general | solution.py:54
  188.8 0.0 all-gather.2.cloned.1.call-update
  188.8 75.8 %reduce-scatter.3.cloned.1.call-done = f32[192,768]{1,0:T(8,128)} async-done(((f32[3072,768]{1,0:T(8,128)}), f32[192,768]{1,0:T(8,128)}) %reduce-scatter.3.cloned.1.call-update) | async-done | bytes 589840 | tf_op jit(solution)/shard_map/reduce_scatter | solution.py:46
  264.6 2.1 multiply_add_fusion.1
  266.7 82.0 %reduce-scatter.5.cloned.1.call-done = f32[192,768]{1,0:T(8,128)} async-done(((f32[3072,768]{1,0:T(8,128)}), f32[192,768]{1,0:T(8,128)}) %reduce-scatter.5.cloned.1.call-update) | async-done | bytes 589840 | tf_op jit(solution)/shard_map/reduce_scatter | solution.py:47
  348.8 2.1 multiply_add_fusion
  350.9 52.6 %all-gather.2.cloned.1.call-done = f32[3072,768]{1,0:T(8,128)} async-done(((f32[192,768]{1,0:T(8,128)}), f32[3072,768]{1,0:T(8,128)}) %all-gather.2.cloned.1.call-update) | async-done | bytes 9437200 | tf_op jit(solution)/shard_map/all_gather | solution.py:55
  403.5 8.0 %copy.18 = f32[4,768,768]{2,1,0:T(8,128)} copy(f32[4,768,768]{2,1,0:T(8,128)} %bitcast.54) | data formatting | bytes 18874368
  (20 shorter events, 0.0 us)
Async XLA Ops:
  7.2 1.9 copy-start
  7.2 173.3 %all-reduce.2.cloned.1.call-start = ((), (), s32[]{:S(2)}) async-start(), calls=%async_computation.2 | async-start | bytes 18874368 | tf_op jit(solution)/shard_map/psum | solution.py:48
  9.1 4.2 %copy-start.1 = (bf16[4,768,768]{2,1,0:T(8,128)(2,1)S(1)}, bf16[4,768,768]{2,1,0:T(8,128)(2,1)}, u32[]{:S(2)}) copy-start(bf16[4,768,768]{2,1,0:T(8,128)(2,1)} %param.9) | copy-start | bytes 14155780
  13.3 30.8 %copy-start.9 = (bf16[2048,768]{1,0:T(8,128)(2,1)}, bf16[2048,768]{1,0:T(8,128)(2,1)S(1)}, u32[]{:S(2)}) copy-start(bf16[2048,768]{1,0:T(8,128)(2,1)S(1)} %convolution_convert_fusion.4) | copy-start | bytes 9437188
  17.5 17.2 %copy-start.13 = (bf16[2048,768]{1,0:T(8,128)(2,1)}, bf16[2048,768]{1,0:T(8,128)(2,1)S(1)}, u32[]{:S(2)}) copy-start(bf16[2048,768]{1,0:T(8,128)(2,1)S(1)} %convolution_convert_fusion.3) | copy-start | bytes 9437188
  17.5 4.2 %copy-start.2 = (bf16[2048,768]{1,0:T(8,128)(2,1)S(1)}, bf16[2048,768]{1,0:T(8,128)(2,1)}, u32[]{:S(2)}) copy-start(bf16[2048,768]{1,0:T(8,128)(2,1)} %param.8) | copy-start | bytes 9437188
  21.7 3.4 copy-start.11
  31.4 3.4 copy-start.3
  40.8 3.4 copy-start.5
  50.1 2.7 copy-start.7
  57.0 207.6 %reduce-scatter.3.cloned.1.call-start = ((), (), s32[]{:S(2)}) async-start(), calls=%async_computation.4 | async-start | bytes 10027008 | tf_op jit(solution)/shard_map/reduce_scatter | solution.py:46
  65.8 2.7 copy-start.10
  68.6 5.0 %copy-start.14 = (bf16[2048,768]{1,0:T(8,128)(2,1)S(1)}, bf16[2048,768]{1,0:T(8,128)(2,1)}, u32[]{:S(2)}) copy-start(bf16[2048,768]{1,0:T(8,128)(2,1)} %copy-done.13) | copy-start | bytes 9437188
  73.6 5.0 %copy-start.12 = (bf16[2048,768]{1,0:T(8,128)(2,1)S(1)}, bf16[2048,768]{1,0:T(8,128)(2,1)}, u32[]{:S(2)}) copy-start(bf16[2048,768]{1,0:T(8,128)(2,1)} %copy-done.11) | copy-start | bytes 9437188
  87.8 261.0 %reduce-scatter.5.cloned.1.call-start = ((), (), s32[]{:S(2)}) async-start(), calls=%async_computation.5 | async-start | bytes 10027008 | tf_op jit(solution)/shard_map/reduce_scatter | solution.py:47
  87.8 5.7 %copy-start.4 = (bf16[2048,768]{1,0:T(8,128)(2,1)S(1)}, bf16[2048,768]{1,0:T(8,128)(2,1)}, u32[]{:S(2)}) copy-start(bf16[2048,768]{1,0:T(8,128)(2,1)} %copy-done.3) | copy-start | bytes 9437188
  93.5 2.8 copy-start.6
  96.3 2.8 copy-start.8
  105.9 297.6 %all-gather.2.cloned.1.call-start = ((), (), s32[]{:S(2)}) async-start(), calls=%async_computation.3 | async-start | bytes 10027008 | tf_op jit(solution)/shard_map/all_gather | solution.py:55
Sparse Core Ops, SparseCore 0:
  57.2 123.3 all-reduce.1
  185.2 79.3 reduce-scatter.2
  269.3 79.4 reduce-scatter.4
  351.4 52.0 all-gather.1
where the time goes:
time: 426 us; the launch traced here: 418 us
  waiting for transfers between devices  285 us (67%)
  matrix products  83.6 us (20%)
  other arithmetic  16.4 us (4%)
  between operations  14.6 us (3%)
  local copies, waits for them, and re-layouts  9.93 us (2%)
  starting transfers between devices  9.16 us (2%)
    reduce_scatter x1, waiting for transfers between devices, device_step(): s_sum = lax.psum_scatter(s_loc, 'data', scatter_dimension=0, tiled=True)  82 us
    reduce_scatter x1, waiting for transfers between devices, device_step(): a_sum = lax.psum_scatter(a_loc, 'data', scatter_dimension=0, tiled=True)  75.8 us
    psum x1, waiting for transfers between devices, device_step(): w_grad = lax.psum(w_loc, 'data')  74.3 us
    all_gather x1, waiting for transfers between devices, device_step(): lax.all_gather(u_rows, 'data', axis=0, tiled=True)  52.6 us
    dot_general x12, matrix products, cross_rows(): jnp.einsum('bi,bj->ij', left_op, right_op, preferred_element_type=jnp.flo...  44.5 us
    dot_general x3, matrix products, local_pass(): jnp.einsum('bj,ij->bi', out_grads[layer_id], weights[layer_id], preferred...  18.2 us
    dot_general x3, matrix products, local_pass(): jnp.dot(layer_inputs[layer_id], weights[layer_id], preferred_element_type...  12.6 us
    unnamed x31, local copies, waits for them, and re-layouts  9.93 us
  transfers between devices with their start and end apart: 4, of which 4 were waited for; matrix products, arithmetic and copies ran while one was open for 12% of the time, Pallas kernels for 0%

commit v1 on v0

v1 whole, which is shorter than its diff:
```python
import jax
import jax.numpy as jnp
from jax import lax
from jax.experimental import pallas as pl
from jax.experimental.pallas import tpu as pltpu
from jax.sharding import PartitionSpec as P

FACTOR_DECAY = 0.75
MESH = pl.DeviceIdType.MESH
F32 = jnp.float32
BF16 = jnp.bfloat16
N_LAYERS = 4
D = 768
STRIP = 192
ROWS = 2048
BLOCK = 512
CHUNK = 256
MBLOCK = 384
PAIR_SLOTS = 2
SLOTS = 7
GELU_C = 0.7978845608028654
GELU_K = 0.044715
CONTRACT_ROWS = (((0,), (0,)), ((), ()))
SCHEDULE = """
F0 F1 F2 B3 B2 P2.3 P2.2 R0 P2.1 R1 B1 R2 S0.1.0 P1.1 S0.1.1 S0.1.2 S1.1.0 P2.0 R3 S1.1.1 S2.1.0 P1.3 R4
S0.2.2 S1.1.2 S1.2.0 S2.1.1 S2.1.2 P1.2 R5 S3.1.0 P0.3 R6 S0.2.0 S0.2.1 S1.2.1 S4.1.0 S3.1.2 P0.0 S1.2.2
S2.2.2 S4.1.1 S3.1.1 S1.3.0 S2.2.0 S5.1.0 S4.1.2 S6.1.0 S6.1.1 S5.1.2 S0.3.2 S3.2.2 S0.3.1 S0.3.0 R7 P0.2
S1.3.1 S4.2.0 S3.2.0 S5.1.1 S6.1.2 S2.2.1 S4.2.2 S4.2.1 S5.2.2 S2.3.2 S1.3.2 R8 P1.0 S3.2.1 S5.2.0 S6.2.0
S6.2.1 S7.1.0 S3.3.2 S2.3.1 S6.2.2 S5.2.1 S4.3.0 S4.3.2 S4.3.1 S7.1.2 S2.3.0 V R9 S3.3.0 S3.3.1 R10 S5.3.0
S6.3.0 S6.3.1 S7.1.1 S8.1.0 P0.1 S5.3.2 S5.3.1 S6.3.2 S7.2.0 S8.1.1 S8.1.2 S7.2.2 S9.1.2 S7.3.2 R11 S9.1.1
S10.1.2 S7.2.1 S7.3.0 S11.1.1 S8.2.1 S10.1.1 S8.2.0 S9.2.1 S11.1.2 U S9.1.0 S10.2.1 S10.1.0 S11.2.1 S8.2.2
S8.3.0 S9.2.2 S11.1.0 f0.2 f0.4 S10.2.2 S8.3.1 f1.4 f2.4 S11.2.2 S9.3.1 f1.2 f2.2 f3.4 S7.3.1 S11.2.0 f0.1
f3.2 f0.6 f2.6 S9.2.0 S8.3.2 S11.3.2 S11.3.0 f1.1 f2.1 S10.2.0 S10.3.2 S10.3.1 f0.5 S11.3.1 f3.1 f2.3 S9.3.2
f3.6 f1.6 S9.3.0 f0.3 f3.5 f1.5 f2.5 f1.3 S10.3.0 f3.3 f2.7 f3.7 f1.7 f0.7
""".split()
PRODUCTS = [(int(e[1]), int(e[3])) for e in SCHEDULE if e[0] == "P"]
N_PROD = len(PRODUCTS)
EARLY = 1
FIRST_LATE = 3
ORDERS = [(1, 2, 4), (2, 4, 1), (4, 1, 2)]
WIDE = 128
PIECES = [(0, 256, (1, 2, 4)), (256, 256, (1, 4, 2)), (512, 256, (2, 1, 4)), (768, 128, (2, 4, 1))]


def xor_chip(chip, mask):
    out = chip
    for bit in (1, 2, 4):
        if mask & bit:
            out = out + bit - 2 * bit * lax.rem(lax.div(chip, bit), 2)
    return out


def unit(j, step, layer, tx):
    bits = {1: tx, 2: layer % 2, 4: layer // 2}
    index = (0, 4, 6)[step]
    for place, dim in enumerate(ORDERS[j][step + 1:]):
        index = index + bits[dim] * (place + 1)
    return index


def cols(j):
    return pl.ds(j * CHUNK, CHUNK)


def kernel(x_hbm, dy_hbm, w_hbm, ainv_hbm, sinv_hbm, u_hbm, a_out, s_out,
           act, wts, part, pair_buf, acc, stg, recv_g, recv_as, gsum, sinv, ainv, vfull, ustrip,
           load_sem, pair_send, pair_recv, credit, send_sem, recv_sem,
           v_send, v_recv, v_fwd_send, v_fwd_recv, v_pair_send, v_pair_recv,
           g_send, g_recv, gp_send, gp_recv, loc_sem):
    me = lax.axis_index("data")
    core = lax.rem(me, 2)
    chip = lax.div(me, 2)
    xbit = lax.rem(chip, 2)
    ybit = lax.rem(lax.div(chip, 2), 2)
    zbit = lax.div(chip, 4)
    layer_own = lax.div(chip, 2)
    partner = chip * 2 + 1 - core

    def peer(mask):
        return xor_chip(chip, mask) * 2 + core

    loads = [
        pltpu.make_async_copy(x_hbm, act.at[0], load_sem.at[0]),
        pltpu.make_async_copy(w_hbm, wts, load_sem.at[1]),
        pltpu.make_async_copy(dy_hbm, act.at[7], load_sem.at[2]),
        pltpu.make_async_copy(ainv_hbm, ainv, load_sem.at[3]),
        pltpu.make_async_copy(sinv_hbm.at[layer_own], sinv, load_sem.at[4]),
    ]
    for ld in loads:
        ld.start()

    barrier = pltpu.get_barrier_semaphore()
    pl.semaphore_signal(barrier, inc=1, device_id=(partner,), device_id_type=MESH)
    for mask in (1, 2, 4):
        pl.semaphore_signal(barrier, inc=1, device_id=(peer(mask),), device_id_type=MESH)
    pl.semaphore_wait(barrier, 4)


    def pair_copy(p, tx):
        row = pl.multiple_of((2 * tx + 1 - core) * STRIP, STRIP)
        return pltpu.make_async_remote_copy(
            src_ref=part.at[p % 2, pl.ds(row, STRIP)],
            dst_ref=pair_buf.at[p % PAIR_SLOTS, tx],
            send_sem=pair_send.at[p % 2, tx],
            recv_sem=pair_recv.at[p % PAIR_SLOTS, tx],
            device_id=(partner,),
            device_id_type=MESH,
        )

    def landing(kind, j, u):
        return recv_g.at[j, u] if kind == 2 else recv_as.at[kind, j, u]

    def staged(p, tx, j):
        if p < FIRST_LATE:
            return stg, (sum(k != 2 for k, _ in PRODUCTS[:p]), tx, slice(None), cols(j))
        n = sum(k != 2 for k, _ in PRODUCTS[FIRST_LATE:p])
        return wts, (n // 2, pl.ds((n % 2) * 2 * STRIP + tx * STRIP, STRIP), cols(j))

    def strip_copy(p, j, step, tx):
        kind, layer = PRODUCTS[p]
        u = unit(j, step, layer, tx)
        if kind == 2:
            src = acc.at[p % SLOTS, tx, :, cols(j)]
        else:
            ref, idx = staged(p, tx, j)
            src = ref.at[idx]
        return pltpu.make_async_remote_copy(
            src_ref=src,
            dst_ref=landing(kind, j, u),
            send_sem=send_sem.at[p % SLOTS, j, tx],
            recv_sem=recv_sem.at[kind, j, u],
            device_id=(peer(ORDERS[j][step]),),
            device_id_type=MESH,
        )

    def product(p):
        kind, layer = PRODUCTS[p]
        left = layer if kind != 1 else 4 + layer
        right = layer if kind == 0 else 4 + layer

        def body(mb, carry):
            ms = pl.ds(pl.multiple_of(mb * MBLOCK, MBLOCK), MBLOCK)
            part[p % 2, ms] = lax.dot_general(act[left, :, ms], act[right], CONTRACT_ROWS,
                                              preferred_element_type=F32)
            return carry
        lax.fori_loop(0, D // MBLOCK, body, 0)
        if p >= PAIR_SLOTS:
            pl.semaphore_wait(credit, 1)
        for tx in range(2):
            pair_copy(p, tx).start()

    def drain(p):
        _, layer = PRODUCTS[p]
        for j in range(3):
            strip_copy(p, j, 0, 1 - xbit).wait_send()

        @pl.when(layer_own != layer)
        def _():
            for j in range(3):
                strip_copy(p, j, 0, xbit).wait_send()

    def equal(dim, layer):
        z_l, y_l = divmod(layer, 2)
        return ybit == y_l if dim == 2 else zbit == z_l

    def stage(p, step, chunks=(0, 1, 2)):
        kind, layer = PRODUCTS[p]
        slot = p % SLOTS
        for j in chunks:
            order = ORDERS[j]
            before = order[:step]
            active = None
            for dim in before:
                if dim != 1:
                    cond = equal(dim, layer)
                    active = cond if active is None else jnp.logical_and(active, cond)
            strips = [xbit] if 1 in before else [0, 1]

            def body(j=j, order=order, strips=strips):
                if step > 0:
                    for tx in strips:
                        strip_copy(p, j, step - 1, tx).wait_recv()
                        u = unit(j, step - 1, layer, tx)
                        got = recv_g[j, u] if kind == 2 else recv_as[kind, j, u].astype(F32)
                        new = acc[slot, tx, :, cols(j)] + got
                        if step < 3:
                            acc[slot, tx, :, cols(j)] = new
                        if kind != 2 and step < 3:
                            ref, idx = staged(p, tx, j)
                            ref[idx] = new.astype(BF16)
                if step == 3:
                    if kind == 2:
                        gsum[:, cols(j)] = new * (1.0 / (ROWS * 16))
                    elif kind == 0:
                        a_out[:, cols(j)] = new
                    else:
                        s_out[:, cols(j)] = new
                    return
                dim = order[step]
                if dim == 1:
                    strip_copy(p, j, step, 1 - xbit).start()
                else:
                    @pl.when(jnp.logical_not(equal(dim, layer)))
                    def _():
                        for tx in strips:
                            strip_copy(p, j, step, tx).start()

            if active is None:
                body()
            else:
                pl.when(active)(body)
    def pair_sum(p):
        kind, layer = PRODUCTS[p]
        slot = p % SLOTS
        if p >= SLOTS:
            drain(p - SLOTS)
        for tx in range(2):
            pair_copy(p, tx).wait_recv()
            row = pl.multiple_of((2 * tx + core) * STRIP, STRIP)
            total = part[p % 2, pl.ds(row, STRIP)] + pair_buf[p % PAIR_SLOTS, tx]
            acc[slot, tx] = total
            if kind != 2:
                for j in range(3):
                    ref, idx = staged(p, tx, j)
                    ref[idx] = total[:, j * CHUNK:(j + 1) * CHUNK].astype(BF16)
        stage(p, 0)
        for tx in range(2):
            pair_copy(p, tx).wait_send()
        if p + PAIR_SLOTS < N_PROD:
            pl.semaphore_signal(credit, inc=1, device_id=(partner,), device_id_type=MESH)


    def forward(layer):
        def body(rb, carry):
            rows = pl.ds(pl.multiple_of(rb * BLOCK, BLOCK), BLOCK)
            z = jnp.dot(act[layer, rows], wts[layer], preferred_element_type=F32).astype(BF16)
            act[4 + layer, rows] = z
            act[layer + 1, rows] = jax.nn.gelu(z.astype(F32), approximate=True).astype(BF16)
            return carry
        lax.fori_loop(0, ROWS // BLOCK, body, 0)

    def backward(layer):
        def body(rb, carry):
            rows = pl.ds(pl.multiple_of(rb * BLOCK, BLOCK), BLOCK)
            d_act = lax.dot_general(act[4 + layer, rows], wts[layer], (((1,), (1,)), ((), ())),
                                    preferred_element_type=F32).astype(BF16).astype(F32)
            z = act[3 + layer, rows].astype(F32)
            z2 = z * z
            t = jnp.tanh(GELU_C * (z + GELU_K * (z2 * z)))
            slope = 0.5 * (1.0 + t) + (0.5 * z) * ((1.0 - t * t) * (GELU_C * (1.0 + 3.0 * GELU_K * z2)))
            act[3 + layer, rows] = (d_act * slope).astype(BF16)
            return carry
        lax.fori_loop(0, ROWS // BLOCK, body, 0)


    my_strip = 2 * xbit + core
    pair_strip = 2 * xbit + 1 - core
    far_strip = 2 * (1 - xbit) + core
    far_pair_strip = 2 * (1 - xbit) + 1 - core
    far = peer(1)

    def vblock(strip, j):
        return vfull.at[pl.ds(pl.multiple_of(strip * STRIP, STRIP), STRIP), cols(j)]

    def vcopy(strip, j, ssem, rsem, dev):
        return pltpu.make_async_remote_copy(
            src_ref=vblock(strip, j), dst_ref=vblock(strip, j), send_sem=ssem.at[j], recv_sem=rsem.at[j],
            device_id=(dev,), device_id_type=MESH)

    def v_stage():
        loads[3].wait()
        loads[4].wait()
        for j in range(3):
            vfull[pl.ds(pl.multiple_of(my_strip * STRIP, STRIP), STRIP), cols(j)] = jnp.dot(
                gsum[...], sinv[:, cols(j)], precision=lax.Precision.HIGHEST, preferred_element_type=F32)
            vcopy(my_strip, j, v_send, v_recv, far).start()
            vcopy(my_strip, j, v_pair_send, v_pair_recv, partner).start()

    def u_block(dev, n):
        first, width, _ = PIECES[n]
        return u_hbm.at[pl.ds(pl.multiple_of(dev * STRIP, STRIP), STRIP), pl.ds(first, width)]

    def u_own(n):
        first, width, _ = PIECES[n]
        return ustrip.at[:, pl.ds(first, width)]

    def u_copy(n, dev, src_own, ssem, rsem, target):
        return pltpu.make_async_remote_copy(
            src_ref=u_own(n) if src_own else u_block(dev, n), dst_ref=u_block(dev, n), send_sem=ssem, recv_sem=rsem,
            device_id=(target,), device_id_type=MESH)

    sent = []

    def launch(n, mask, dims):
        dev = peer(mask) if mask else me
        for d in dims:
            m = mask | d
            cp = u_copy(n, dev, mask == 0, g_send.at[n, m], g_recv.at[n, m], peer(d))
            cp.start()
            sent.append(cp)
        cp = u_copy(n, dev, mask == 0, gp_send.at[n, mask], gp_recv.at[n, mask], partner)
        cp.start()
        sent.append(cp)

    local = [pltpu.make_async_copy(u_own(n), u_block(me, n), loc_sem.at[n]) for n in range(4)]

    def u_stage():
        for j in range(3):
            vcopy(far_strip, j, v_send, v_recv, far).wait_recv()
            vcopy(far_strip, j, v_fwd_send, v_fwd_recv, partner).start()
        for j in range(3):
            vcopy(pair_strip, j, v_pair_send, v_pair_recv, partner).wait_recv()
            vcopy(far_pair_strip, j, v_fwd_send, v_fwd_recv, partner).wait_recv()
            u_rows = jnp.dot(ainv[...], vfull[:, cols(j)], precision=lax.Precision.HIGHEST, preferred_element_type=F32)
            high = u_rows.astype(BF16)
            ustrip[:, cols(j)] = high
            pieces = [j]
            if j == 2:
                ustrip[:, D:] = (u_rows - high.astype(F32))[:, CHUNK - WIDE:].astype(BF16)
                pieces = [2, 3]
            for n in pieces:
                launch(n, 0, PIECES[n][2])
                local[n].start()

    def u_forward(n, mask):
        order = PIECES[n][2]
        last = max(i for i in range(3) if mask & order[i])
        u_copy(n, peer(mask), False, g_send.at[n, mask], g_recv.at[n, mask], peer(order[last])).wait_recv()
        launch(n, mask, order[last + 1:])


    waited = set()

    def loaded(n):
        if n not in waited:
            waited.add(n)
            loads[n].wait()

    loaded(0)
    n_prod = 0
    for event in SCHEDULE:
        what, args = event[0], [int(a) for a in event[1:].split(".") if a]
        if what == "P":
            if args[0] == 1 or (args[0] == 2 and args[1] == 3):
                loaded(2)
            product(n_prod)
            n_prod += 1
        elif what == "R":
            pair_sum(args[0])
        elif what == "S":
            stage(args[0], args[1], (args[2],))
        elif what == "F":
            loaded(1)
            forward(args[0])
        elif what == "B":
            loaded(2)
            backward(args[0])
        elif what == "V":
            v_stage()
        elif what == "U":
            u_stage()
        else:
            u_forward(*args)
    for n in range(4):
        for mask in range(8):
            dev = xor_chip(chip, mask) * 2 + 1 - core
            u_copy(n, dev, False, gp_send.at[n, mask], gp_recv.at[n, mask], partner).wait_recv()
    for cp in sent:
        cp.wait_send()
    for cp in local:
        cp.wait()
    for j in range(3):
        vcopy(my_strip, j, v_send, v_recv, far).wait_send()
        vcopy(my_strip, j, v_pair_send, v_pair_recv, partner).wait_send()
        vcopy(far_strip, j, v_fwd_send, v_fwd_recv, partner).wait_send()
    for p in range(N_PROD - SLOTS, N_PROD):
        drain(p)


def solution(mesh):
    dma = pltpu.SemaphoreType.DMA
    any_spec = pl.BlockSpec(memory_space=pl.ANY)
    vmem_spec = pl.BlockSpec(memory_space=pltpu.VMEM)

    def device_step(x_loc, dy_loc, weights, a_old_rows, s_old_rows, a_inv_rows, s_inv):
        u_parts, a_sum, s_sum = pl.pallas_call(
            kernel,
            out_shape=(
                jax.ShapeDtypeStruct((N_LAYERS * D, D + WIDE), BF16),
                jax.ShapeDtypeStruct((STRIP, D), F32),
                jax.ShapeDtypeStruct((STRIP, D), F32),
            ),
            in_specs=[any_spec] * 5,
            out_specs=(any_spec, vmem_spec, vmem_spec),
            scratch_shapes=[
                pltpu.VMEM((8, ROWS, D), BF16),
                pltpu.VMEM((N_LAYERS, D, D), BF16),
                pltpu.VMEM((2, D, D), F32),
                pltpu.VMEM((PAIR_SLOTS, 2, STRIP, D), F32),
                pltpu.VMEM((SLOTS, 2, STRIP, D), F32),
                pltpu.VMEM((EARLY, 2, STRIP, D), BF16),
                pltpu.VMEM((3, 7, STRIP, CHUNK), F32),
                pltpu.VMEM((2, 3, 7, STRIP, CHUNK), BF16),
                pltpu.VMEM((STRIP, D), F32),
                pltpu.VMEM((D, D), F32),
                pltpu.VMEM((STRIP, D), F32),
                pltpu.VMEM((D, D), F32),
                pltpu.VMEM((STRIP, D + WIDE), BF16),
                dma((5,)), dma((2, 2)), dma((PAIR_SLOTS, 2)), pltpu.SemaphoreType.REGULAR,
                dma((SLOTS, 3, 2)), dma((3, 3, 7)),
                dma((3,)), dma((3,)), dma((3,)), dma((3,)), dma((3,)), dma((3,)),
                dma((4, 8)), dma((4, 8)), dma((4, 8)), dma((4, 8)), dma((4,)),
            ],
            compiler_params=pltpu.CompilerParams(
                collective_id=0, has_side_effects=True, vmem_limit_bytes=67043328),
        )(x_loc, dy_loc, weights, a_inv_rows, s_inv)
        scale = (1.0 - FACTOR_DECAY) / (ROWS * 16)
        a_new = FACTOR_DECAY * a_old_rows + scale * a_sum
        s_new = FACTOR_DECAY * s_old_rows + scale * s_sum
        u_flat = u_parts[:, :D].astype(F32) + jnp.pad(u_parts[:, D:].astype(F32), ((0, 0), (D - WIDE, 0)))
        return u_flat.reshape(N_LAYERS, D, D), a_new, s_new

    row_spec = P("data", None)
    return jax.shard_map(
        device_step,
        mesh=mesh,
        in_specs=(row_spec, row_spec, P(), row_spec, row_spec, row_spec, P()),
        out_specs=(P(), row_spec, row_spec),
        check_vma=False,
    )
```

time: 426 us -> 148 us (0.35); the launches traced: 418 us -> 148 us
  waiting for transfers between devices: 285 us -> 0 us
  Pallas kernels: 0 us -> 136 us
  matrix products: 83.6 us -> 0 us
  between operations: 14.6 us -> 0.64 us
  starting transfers between devices: 9.16 us -> 0 us
  local copies, waits for them, and re-layouts: 9.93 us -> 1.18 us
  other arithmetic: 16.4 us -> 9.64 us
    reduce_scatter x2 -> x0, waiting for transfers between devices: 158 us -> none  [the longest x1 82 us: device_step(): s_sum = lax.psum_scatter(s_loc, 'data', scatter_dimension=0, tiled=True)]
    pallas_call x0 -> x1, Pallas kernels: none -> 136 us  [device_step(): pl.pallas_call(kernel, out_shape=(jax.ShapeDtypeStruct((N_LAYERS * D, D +...]
    dot_general x20 -> x0, matrix products: 83.6 us -> none  [the longest x12 44.5 us: cross_rows(): jnp.einsum('bi,bj->ij', left_op, right_op, preferred_element_type=jnp.flo...]
    psum x1 -> x0, waiting for transfers between devices: 74.3 us -> none  [device_step(): w_grad = lax.psum(w_loc, 'data')]
    all_gather x1 -> x0, waiting for transfers between devices: 52.6 us -> none  [device_step(): lax.all_gather(u_rows, 'data', axis=0, tiled=True)]
    div x3 -> x0, other arithmetic: 12.1 us -> none  [the longest x1 4.19 us: device_step(): jnp.stack([cross_rows(h_in, g_out) for h_in, g_out in zip(layer_inputs, o...]
    unnamed x31 -> x0, local copies, waits for them, and re-layouts: 9.93 us -> none
    reduce_scatter x2 -> x0, starting transfers between devices: 8.83 us -> none  [the longest x1 8.79 us: device_step(): a_sum = lax.psum_scatter(a_loc, 'data', scatter_dimension=0, tiled=True)]
  transfers between devices with their start and end apart: 4 -> 0, of which waited for: 4 -> 0; matrix products, arithmetic and copies ran while one was open for 12% -> 0% of each run, Pallas kernels for 0% -> 0%
where the time goes in v1:
time: 148 us
  Pallas kernels  136 us (92%)
  other arithmetic  9.64 us (7%)
    pallas_call x1, Pallas kernels, device_step(): pl.pallas_call(kernel, out_shape=(jax.ShapeDtypeStruct((N_LAYERS * D, D +...  136 us
    add x1, other arithmetic, device_step(): u_parts[:, :D].astype(F32)  6.89 us

profile of v1, /device:TPU:0, one launch (start us, length us, event | category | flops | bytes accessed | tf_op | source)
XLA Modules:
  0.0 147.9 jit_solution(1613747516644752350)
XLA Ops:
  0.6 136.5 %shard_map.94 = (bf16[3072,896]{1,0:T(8,128)(2,1)}, f32[192,768]{1,0:T(8,128)}, f32[192,768]{1,0:T(8,128)}) custom-call(bf16[2048,768]{1,0:T(8,128)(2,1)} %x_hbm.1, bf16[2048,768]{1,0:T(8,128)(2,1)} %dy_hbm.1, bf16[4,768,768]{2,1,0:T(8,128)(2,1)} %w_hbm.1, f32[192,768]{1,0:T(8,128)} %ainv_hbm.1, f32[4,768,768]{2,1,0:T(8,128)} %sinv_hbm.1), custom_call_target="tpu_custom_call" | custom-call | tf_op jit(solution)/shard_map/pallas_call | solution.py:386
  137.1 2.8 %multiply_add_fusion = (f32[192,768]{1,0:T(8,128)}, f32[192,768]{1,0:T(8,128)}) fusion(f32[192,768]{1,0:T(8,128)} %get-tuple-element.8, f32[192,768]{1,0:T(8,128)} %param.11, f32[192,768]{1,0:T(8,128)} %get-tuple-element.7, f32[192,768]{1,0:T(8,128)} %param.10), kind=kLoop, calls=%fused_computation.1 | loop fusion | flops 884736 | bytes 3538944 | tf_op jit(solution)/shard_map/add | solution.py:419
  139.9 1.2 slice.7
  141.1 6.9 %convert_add_fusion = f32[3072,768]{1,0:T(8,128)} fusion(bf16[3072,128]{1,0:T(8,128)(2,1)S(1)} %slice.7, bf16[3072,896]{1,0:T(8,128)(2,1)} %get-tuple-element.6), kind=kLoop, calls=%fused_computation | loop fusion | flops 7077888 | bytes 14942208 | tf_op jit(solution)/shard_map/add | solution.py:420

commit v2 on v1

--- a/solution.py
+++ b/solution.py
@@ -17,29 +17,44 @@
 CHUNK = 256
 MBLOCK = 384
 PAIR_SLOTS = 2
+TAIL_STEPS = 4
 SLOTS = 7
 GELU_C = 0.7978845608028654
 GELU_K = 0.044715
 CONTRACT_ROWS = (((0,), (0,)), ((), ()))
-SCHEDULE = """
-F0 F1 F2 B3 B2 P2.3 P2.2 R0 P2.1 R1 B1 R2 S0.1.0 P1.1 S0.1.1 S0.1.2 S1.1.0 P2.0 R3 S1.1.1 S2.1.0 P1.3 R4
-S0.2.2 S1.1.2 S1.2.0 S2.1.1 S2.1.2 P1.2 R5 S3.1.0 P0.3 R6 S0.2.0 S0.2.1 S1.2.1 S4.1.0 S3.1.2 P0.0 S1.2.2
-S2.2.2 S4.1.1 S3.1.1 S1.3.0 S2.2.0 S5.1.0 S4.1.2 S6.1.0 S6.1.1 S5.1.2 S0.3.2 S3.2.2 S0.3.1 S0.3.0 R7 P0.2
-S1.3.1 S4.2.0 S3.2.0 S5.1.1 S6.1.2 S2.2.1 S4.2.2 S4.2.1 S5.2.2 S2.3.2 S1.3.2 R8 P1.0 S3.2.1 S5.2.0 S6.2.0
-S6.2.1 S7.1.0 S3.3.2 S2.3.1 S6.2.2 S5.2.1 S4.3.0 S4.3.2 S4.3.1 S7.1.2 S2.3.0 V R9 S3.3.0 S3.3.1 R10 S5.3.0
-S6.3.0 S6.3.1 S7.1.1 S8.1.0 P0.1 S5.3.2 S5.3.1 S6.3.2 S7.2.0 S8.1.1 S8.1.2 S7.2.2 S9.1.2 S7.3.2 R11 S9.1.1
-S10.1.2 S7.2.1 S7.3.0 S11.1.1 S8.2.1 S10.1.1 S8.2.0 S9.2.1 S11.1.2 U S9.1.0 S10.2.1 S10.1.0 S11.2.1 S8.2.2
-S8.3.0 S9.2.2 S11.1.0 f0.2 f0.4 S10.2.2 S8.3.1 f1.4 f2.4 S11.2.2 S9.3.1 f1.2 f2.2 f3.4 S7.3.1 S11.2.0 f0.1
-f3.2 f0.6 f2.6 S9.2.0 S8.3.2 S11.3.2 S11.3.0 f1.1 f2.1 S10.2.0 S10.3.2 S10.3.1 f0.5 S11.3.1 f3.1 f2.3 S9.3.2
-f3.6 f1.6 S9.3.0 f0.3 f3.5 f1.5 f2.5 f1.3 S10.3.0 f3.3 f2.7 f3.7 f1.7 f0.7
-""".split()
-PRODUCTS = [(int(e[1]), int(e[3])) for e in SCHEDULE if e[0] == "P"]
+SCHEDULE = [
+    ("F", 0), ("F", 1), ("F", 2), ("B", 3), ("B", 2), ("P", 0, 0), ("P", 2, 2), ("R", 0), ("P", 2, 3), ("R", 1),
+    ("P", 2, 1), ("R", 2), ("S", 0, 1, 0), ("S", 0, 1, 1), ("S", 0, 1, 2), ("B", 1), ("R", 3), ("S", 1, 1, 0),
+    ("P", 2, 0), ("S", 1, 1, 1), ("S", 1, 1, 2), ("S", 2, 1, 0), ("S", 0, 2, 1), ("P", 1, 2), ("R", 4),
+    ("S", 2, 1, 1), ("S", 0, 2, 0), ("S", 0, 2, 2), ("P", 1, 3), ("R", 5), ("S", 1, 2, 0), ("S", 1, 2, 2),
+    ("S", 2, 1, 2), ("S", 3, 1, 0), ("S", 3, 1, 2), ("S", 0, 3, 1), ("P", 0, 2), ("R", 6), ("S", 3, 1, 1),
+    ("P", 0, 1), ("S", 4, 1, 0), ("S", 4, 1, 1), ("S", 5, 1, 0), ("S", 2, 2, 0), ("S", 2, 2, 1), ("S", 1, 2, 1),
+    ("S", 4, 1, 2), ("S", 0, 3, 2), ("S", 3, 2, 2), ("S", 0, 3, 0), ("R", 7), ("P", 1, 1), ("S", 2, 2, 2),
+    ("S", 3, 2, 0), ("S", 5, 1, 1), ("S", 5, 1, 2), ("S", 6, 1, 0), ("S", 1, 3, 2), ("S", 1, 3, 0), ("S", 1, 3, 1),
+    ("R", 8), ("P", 1, 0), ("S", 4, 2, 0), ("S", 4, 2, 2), ("S", 6, 1, 1), ("S", 6, 1, 2), ("S", 2, 3, 1),
+    ("S", 3, 2, 1), ("S", 4, 2, 1), ("S", 5, 2, 0), ("S", 7, 1, 0), ("S", 2, 3, 2), ("S", 2, 3, 0), ("R", 9),
+    ("S", 5, 2, 2), ("P", 0, 3), ("S", 3, 3, 2), ("S", 3, 3, 0), ("S", 8, 1, 0), ("S", 7, 1, 2), ("S", 6, 2, 2),
+    ("S", 7, 1, 1), ("S", 6, 2, 0), ("S", 4, 3, 1), ("S", 3, 3, 1), ("R", 10), ("S", 8, 1, 2), ("S", 8, 1, 1),
+    ("S", 9, 1, 0), ("S", 4, 3, 0), ("S", 4, 3, 2), ("V",), ("R", 11), ("S", 5, 2, 1), ("S", 6, 2, 1),
+    ("S", 7, 2, 0), ("S", 7, 2, 2), ("S", 5, 3, 2), ("S", 5, 3, 0), ("S", 6, 3, 0), ("S", 10, 1, 0), ("S", 9, 1, 2),
+    ("S", 8, 2, 2), ("S", 9, 1, 1), ("S", 8, 2, 0), ("S", 6, 3, 2), ("S", 9, 2, 0), ("S", 10, 1, 1), ("S", 7, 2, 1),
+    ("S", 7, 3, 2), ("S", 10, 1, 2), ("W", 0), ("U", 0), ("S", 10, 2, 0), ("S", 11, 1, 2), ("S", 8, 2, 1),
+    ("S", 11, 1, 1), ("W", 1), ("S", 10, 2, 1), ("S", 7, 3, 0), ("U", 1), ("S", 8, 3, 2), ("S", 9, 2, 1),
+    ("f", 0, 2), ("S", 8, 3, 0), ("W", 2), ("S", 10, 3, 0), ("S", 11, 2, 1), ("U", 2), ("S", 9, 3, 0),
+    ("S", 11, 1, 0), ("f", 1, 2), ("S", 5, 3, 1), ("f", 0, 4), ("S", 6, 3, 1), ("S", 9, 2, 2), ("f", 1, 4),
+    ("S", 7, 3, 1), ("S", 10, 2, 2), ("f", 0, 1), ("f", 2, 2), ("f", 3, 2), ("f", 0, 6), ("S", 8, 3, 1),
+    ("f", 2, 4), ("f", 3, 4), ("S", 9, 3, 2), ("S", 11, 2, 0), ("S", 9, 3, 1), ("f", 1, 6), ("S", 10, 3, 1),
+    ("S", 11, 3, 1), ("S", 11, 2, 2), ("S", 10, 3, 2), ("f", 1, 1), ("f", 0, 5), ("f", 2, 1), ("f", 2, 6),
+    ("f", 0, 3), ("f", 3, 1), ("S", 11, 3, 2), ("f", 3, 6), ("S", 11, 3, 0), ("f", 2, 3), ("f", 1, 3), ("f", 1, 5),
+    ("f", 3, 3), ("f", 2, 5), ("f", 0, 7), ("f", 3, 5), ("f", 2, 7), ("f", 1, 7), ("f", 3, 7),
+]
+PRODUCTS = [event[1:] for event in SCHEDULE if event[0] == "P"]
 N_PROD = len(PRODUCTS)
 EARLY = 1
-FIRST_LATE = 3
+FIRST_LATE = 4
 ORDERS = [(1, 2, 4), (2, 4, 1), (4, 1, 2)]
 WIDE = 128
-PIECES = [(0, 256, (1, 2, 4)), (256, 256, (1, 4, 2)), (512, 256, (2, 1, 4)), (768, 128, (2, 4, 1))]
+PIECES = [(0, 256, (1, 2, 4)), (256, 256, (1, 4, 2)), (512, 256, (2, 4, 1)), (768, 128, (1, 2, 4))]
 
 
 def xor_chip(chip, mask):
@@ -235,7 +250,10 @@
             rows = pl.ds(pl.multiple_of(rb * BLOCK, BLOCK), BLOCK)
             z = jnp.dot(act[layer, rows], wts[layer], preferred_element_type=F32).astype(BF16)
             act[4 + layer, rows] = z
-            act[layer + 1, rows] = jax.nn.gelu(z.astype(F32), approximate=True).astype(BF16)
+            zf = z.astype(F32)
+            half = 0.5 * zf
+            t = jnp.tanh(zf * (GELU_C + (GELU_C * GELU_K) * (zf * zf)))
+            act[layer + 1, rows] = (half + half * t).astype(BF16)
             return carry
         lax.fori_loop(0, ROWS // BLOCK, body, 0)
 
@@ -246,8 +264,8 @@
                                     preferred_element_type=F32).astype(BF16).astype(F32)
             z = act[3 + layer, rows].astype(F32)
             z2 = z * z
-            t = jnp.tanh(GELU_C * (z + GELU_K * (z2 * z)))
-            slope = 0.5 * (1.0 + t) + (0.5 * z) * ((1.0 - t * t) * (GELU_C * (1.0 + 3.0 * GELU_K * z2)))
+            t = jnp.tanh(z * (GELU_C + (GELU_C * GELU_K) * z2))
+            slope = (0.5 + 0.5 * t) + (0.5 * z) * ((1.0 - t * t) * (GELU_C + (3.0 * GELU_C * GELU_K) * z2))
             act[3 + layer, rows] = (d_act * slope).astype(BF16)
             return carry
         lax.fori_loop(0, ROWS // BLOCK, body, 0)
@@ -304,23 +322,23 @@
 
     local = [pltpu.make_async_copy(u_own(n), u_block(me, n), loc_sem.at[n]) for n in range(4)]
 
-    def u_stage():
-        for j in range(3):
-            vcopy(far_strip, j, v_send, v_recv, far).wait_recv()
-            vcopy(far_strip, j, v_fwd_send, v_fwd_recv, partner).start()
-        for j in range(3):
-            vcopy(pair_strip, j, v_pair_send, v_pair_recv, partner).wait_recv()
-            vcopy(far_pair_strip, j, v_fwd_send, v_fwd_recv, partner).wait_recv()
-            u_rows = jnp.dot(ainv[...], vfull[:, cols(j)], precision=lax.Precision.HIGHEST, preferred_element_type=F32)
-            high = u_rows.astype(BF16)
-            ustrip[:, cols(j)] = high
-            pieces = [j]
-            if j == 2:
-                ustrip[:, D:] = (u_rows - high.astype(F32))[:, CHUNK - WIDE:].astype(BF16)
-                pieces = [2, 3]
-            for n in pieces:
-                launch(n, 0, PIECES[n][2])
-                local[n].start()
+    def v_pass(j):
+        vcopy(far_strip, j, v_send, v_recv, far).wait_recv()
+        vcopy(far_strip, j, v_fwd_send, v_fwd_recv, partner).start()
+
+    def u_stage(j):
+        vcopy(pair_strip, j, v_pair_send, v_pair_recv, partner).wait_recv()
+        vcopy(far_pair_strip, j, v_fwd_send, v_fwd_recv, partner).wait_recv()
+        u_rows = jnp.dot(ainv[...], vfull[:, cols(j)], precision=lax.Precision.HIGHEST, preferred_element_type=F32)
+        high = u_rows.astype(BF16)
+        ustrip[:, cols(j)] = high
+        pieces = [j]
+        if j == 2:
+            ustrip[:, D:] = (u_rows - high.astype(F32))[:, CHUNK - WIDE:].astype(BF16)
+            pieces = [2, 3]
+        for n in pieces:
+            launch(n, 0, PIECES[n][2])
+            local[n].start()
 
     def u_forward(n, mask):
         order = PIECES[n][2]
@@ -339,7 +357,7 @@
     loaded(0)
     n_prod = 0
     for event in SCHEDULE:
-        what, args = event[0], [int(a) for a in event[1:].split(".") if a]
+        what, args = event[0], event[1:]
         if what == "P":
             if args[0] == 1 or (args[0] == 2 and args[1] == 3):
                 loaded(2)
@@ -358,7 +376,9 @@
         elif what == "V":
             v_stage()
         elif what == "U":
-            u_stage()
+            u_stage(args[0])
+        elif what == "W":
+            v_pass(args[0])
         else:
             u_forward(*args)
     for n in range(4):
@@ -375,6 +395,14 @@
         vcopy(far_strip, j, v_fwd_send, v_fwd_recv, partner).wait_send()
     for p in range(N_PROD - SLOTS, N_PROD):
         drain(p)
+
+
+def tail(u_ref, a_old, a_sum, s_old, s_sum, u_out, a_new, s_new):
+    scale = (1.0 - FACTOR_DECAY) / (ROWS * 16)
+    u_out[:, :D - WIDE] = u_ref[:, :D - WIDE].astype(F32)
+    u_out[:, D - WIDE:] = u_ref[:, D - WIDE:D].astype(F32) + u_ref[:, D:].astype(F32)
+    a_new[...] = FACTOR_DECAY * a_old[...] + scale * a_sum[...]
+    s_new[...] = FACTOR_DECAY * s_old[...] + scale * s_sum[...]
 
 
 def solution(mesh):
@@ -414,10 +442,20 @@
             compiler_params=pltpu.CompilerParams(
                 collective_id=0, has_side_effects=True, vmem_limit_bytes=67043328),
         )(x_loc, dy_loc, weights, a_inv_rows, s_inv)
-        scale = (1.0 - FACTOR_DECAY) / (ROWS * 16)
-        a_new = FACTOR_DECAY * a_old_rows + scale * a_sum
-        s_new = FACTOR_DECAY * s_old_rows + scale * s_sum
-        u_flat = u_parts[:, :D].astype(F32) + jnp.pad(u_parts[:, D:].astype(F32), ((0, 0), (D - WIDE, 0)))
+        u_block = pl.BlockSpec((N_LAYERS * D // TAIL_STEPS, D + WIDE), lambda i: (i, 0))
+        out_block = pl.BlockSpec((N_LAYERS * D // TAIL_STEPS, D), lambda i: (i, 0))
+        row_block = pl.BlockSpec((STRIP // TAIL_STEPS, D), lambda i: (i, 0))
+        u_flat, a_new, s_new = pl.pallas_call(
+            tail,
+            grid=(TAIL_STEPS,),
+            out_shape=(
+                jax.ShapeDtypeStruct((N_LAYERS * D, D), F32),
+                jax.ShapeDtypeStruct((STRIP, D), F32),
+                jax.ShapeDtypeStruct((STRIP, D), F32),
+            ),
+            in_specs=[u_block] + [row_block] * 4,
+            out_specs=(out_block, row_block, row_block),
+        )(u_parts, a_old_rows, a_sum, s_old_rows, s_sum)
         return u_flat.reshape(N_LAYERS, D, D), a_new, s_new
 
     row_spec = P("data", None)

time: 148 us -> 137 us (0.926)
  other arithmetic: 9.64 us -> 0 us
    add x2 -> x0, other arithmetic: 9.64 us -> none  [the longest x1 6.89 us: device_step(): u_parts[:, :D].astype(F32)]
    pallas_call x0 -> x1, Pallas kernels: none -> 7.3 us  [device_step(): pl.pallas_call(tail, grid=(TAIL_STEPS,), out_shape=(jax.ShapeDtypeStruct(...]
    pallas_call x1, Pallas kernels: 136 us -> 129 us  [device_step(): pl.pallas_call(kernel, out_shape=(jax.ShapeDtypeStruct((N_LAYERS * D, D +...]
where the time goes in v2:
time: 137 us
  Pallas kernels  137 us (100%)
    pallas_call x1, Pallas kernels, device_step(): pl.pallas_call(kernel, out_shape=(jax.ShapeDtypeStruct((N_LAYERS * D, D +...  129 us
    pallas_call x1, Pallas kernels, device_step(): pl.pallas_call(tail, grid=(TAIL_STEPS,), out_shape=(jax.ShapeDtypeStruct(...  7.3 us

profile of v2, /device:TPU:0, one launch (start us, length us, event | category | flops | bytes accessed | tf_op | source)
XLA Modules:
  0.0 137.2 jit_solution(14156186817725675356)
XLA Ops:
  0.6 129.3 %shard_map.94 = (bf16[3072,896]{1,0:T(8,128)(2,1)}, f32[192,768]{1,0:T(8,128)}, f32[192,768]{1,0:T(8,128)}) custom-call(bf16[2048,768]{1,0:T(8,128)(2,1)} %x_hbm.1, bf16[2048,768]{1,0:T(8,128)(2,1)} %dy_hbm.1, bf16[4,768,768]{2,1,0:T(8,128)(2,1)} %w_hbm.1, f32[192,768]{1,0:T(8,128)} %ainv_hbm.1, f32[4,768,768]{2,1,0:T(8,128)} %sinv_hbm.1), custom_call_target="tpu_custom_call" | custom-call | tf_op jit(solution)/shard_map/pallas_call | solution.py:414
  129.9 7.3 %shard_map.95 = (f32[3072,768]{1,0:T(8,128)}, f32[192,768]{1,0:T(8,128)}, f32[192,768]{1,0:T(8,128)}) custom-call(bf16[3072,896]{1,0:T(8,128)(2,1)} %get-tuple-element.9.u_ref, f32[192,768]{1,0:T(8,128)} %a_old.1, f32[192,768]{1,0:T(8,128)} %get-tuple-element.10.a_sum, f32[192,768]{1,0:T(8,128)} %s_old.1, f32[192,768]{1,0:T(8,128)} %get-tuple-element.11.s_sum), custom_call_target="tpu_custom_call" | custom-call | tf_op jit(solution)/shard_map/pallas_call | solution.py:448

commit v3 on v2

--- a/solution.py
+++ b/solution.py
@@ -23,32 +23,21 @@
 GELU_K = 0.044715
 CONTRACT_ROWS = (((0,), (0,)), ((), ()))
 SCHEDULE = [
-    ("F", 0), ("F", 1), ("F", 2), ("B", 3), ("B", 2), ("P", 0, 0), ("P", 2, 2), ("R", 0), ("P", 2, 3), ("R", 1),
-    ("P", 2, 1), ("R", 2), ("S", 0, 1, 0), ("S", 0, 1, 1), ("S", 0, 1, 2), ("B", 1), ("R", 3), ("S", 1, 1, 0),
-    ("P", 2, 0), ("S", 1, 1, 1), ("S", 1, 1, 2), ("S", 2, 1, 0), ("S", 0, 2, 1), ("P", 1, 2), ("R", 4),
-    ("S", 2, 1, 1), ("S", 0, 2, 0), ("S", 0, 2, 2), ("P", 1, 3), ("R", 5), ("S", 1, 2, 0), ("S", 1, 2, 2),
-    ("S", 2, 1, 2), ("S", 3, 1, 0), ("S", 3, 1, 2), ("S", 0, 3, 1), ("P", 0, 2), ("R", 6), ("S", 3, 1, 1),
-    ("P", 0, 1), ("S", 4, 1, 0), ("S", 4, 1, 1), ("S", 5, 1, 0), ("S", 2, 2, 0), ("S", 2, 2, 1), ("S", 1, 2, 1),
-    ("S", 4, 1, 2), ("S", 0, 3, 2), ("S", 3, 2, 2), ("S", 0, 3, 0), ("R", 7), ("P", 1, 1), ("S", 2, 2, 2),
-    ("S", 3, 2, 0), ("S", 5, 1, 1), ("S", 5, 1, 2), ("S", 6, 1, 0), ("S", 1, 3, 2), ("S", 1, 3, 0), ("S", 1, 3, 1),
-    ("R", 8), ("P", 1, 0), ("S", 4, 2, 0), ("S", 4, 2, 2), ("S", 6, 1, 1), ("S", 6, 1, 2), ("S", 2, 3, 1),
-    ("S", 3, 2, 1), ("S", 4, 2, 1), ("S", 5, 2, 0), ("S", 7, 1, 0), ("S", 2, 3, 2), ("S", 2, 3, 0), ("R", 9),
-    ("S", 5, 2, 2), ("P", 0, 3), ("S", 3, 3, 2), ("S", 3, 3, 0), ("S", 8, 1, 0), ("S", 7, 1, 2), ("S", 6, 2, 2),
-    ("S", 7, 1, 1), ("S", 6, 2, 0), ("S", 4, 3, 1), ("S", 3, 3, 1), ("R", 10), ("S", 8, 1, 2), ("S", 8, 1, 1),
-    ("S", 9, 1, 0), ("S", 4, 3, 0), ("S", 4, 3, 2), ("V",), ("R", 11), ("S", 5, 2, 1), ("S", 6, 2, 1),
-    ("S", 7, 2, 0), ("S", 7, 2, 2), ("S", 5, 3, 2), ("S", 5, 3, 0), ("S", 6, 3, 0), ("S", 10, 1, 0), ("S", 9, 1, 2),
-    ("S", 8, 2, 2), ("S", 9, 1, 1), ("S", 8, 2, 0), ("S", 6, 3, 2), ("S", 9, 2, 0), ("S", 10, 1, 1), ("S", 7, 2, 1),
-    ("S", 7, 3, 2), ("S", 10, 1, 2), ("W", 0), ("U", 0), ("S", 10, 2, 0), ("S", 11, 1, 2), ("S", 8, 2, 1),
-    ("S", 11, 1, 1), ("W", 1), ("S", 10, 2, 1), ("S", 7, 3, 0), ("U", 1), ("S", 8, 3, 2), ("S", 9, 2, 1),
-    ("f", 0, 2), ("S", 8, 3, 0), ("W", 2), ("S", 10, 3, 0), ("S", 11, 2, 1), ("U", 2), ("S", 9, 3, 0),
-    ("S", 11, 1, 0), ("f", 1, 2), ("S", 5, 3, 1), ("f", 0, 4), ("S", 6, 3, 1), ("S", 9, 2, 2), ("f", 1, 4),
-    ("S", 7, 3, 1), ("S", 10, 2, 2), ("f", 0, 1), ("f", 2, 2), ("f", 3, 2), ("f", 0, 6), ("S", 8, 3, 1),
-    ("f", 2, 4), ("f", 3, 4), ("S", 9, 3, 2), ("S", 11, 2, 0), ("S", 9, 3, 1), ("f", 1, 6), ("S", 10, 3, 1),
-    ("S", 11, 3, 1), ("S", 11, 2, 2), ("S", 10, 3, 2), ("f", 1, 1), ("f", 0, 5), ("f", 2, 1), ("f", 2, 6),
-    ("f", 0, 3), ("f", 3, 1), ("S", 11, 3, 2), ("f", 3, 6), ("S", 11, 3, 0), ("f", 2, 3), ("f", 1, 3), ("f", 1, 5),
-    ("f", 3, 3), ("f", 2, 5), ("f", 0, 7), ("f", 3, 5), ("f", 2, 7), ("f", 1, 7), ("f", 3, 7),
+    "F0 F1 F2 B3", "B2 P0.0 P2.2 R0", "P2.3 R1 P2.1 R2", "S0.1.0 S0.1.1 S0.1.2 B1", "R3 S1.1.0 P2.0 S1.1.1",
+    "S1.1.2 S2.1.0 S0.2.1 P1.2", "R4 S2.1.1 S0.2.0 S0.2.2", "P1.3 R5 S1.2.0 S1.2.2", "S2.1.2 S3.1.0 S3.1.2 S0.3.1",
+    "P0.2 R6 S3.1.1 P0.1", "S4.1.0 S4.1.1 S5.1.0 S2.2.0", "S2.2.1 S1.2.1 S4.1.2 S0.3.2", "S3.2.2 S0.3.0 R7 P1.1",
+    "S2.2.2 S3.2.0 S5.1.1 S5.1.2", "S6.1.0 S1.3.2 S1.3.0 S1.3.1", "R8 P1.0 S4.2.0 S4.2.2",
+    "S6.1.1 S6.1.2 S2.3.1 S3.2.1", "S4.2.1 S5.2.0 S7.1.0 S2.3.2", "S2.3.0 R9 S5.2.2 P0.3",
+    "S3.3.2 S3.3.0 S8.1.0 S7.1.2", "S6.2.2 S7.1.1 S6.2.0 S4.3.1", "S3.3.1 R10 S8.1.2 S8.1.1",
+    "S9.1.0 S4.3.0 S4.3.2 V", "R11 S5.2.1 S6.2.1 S7.2.0", "S7.2.2 S5.3.2 S5.3.0 S6.3.0",
+    "S10.1.0 S9.1.2 S8.2.2 S9.1.1", "S8.2.0 S6.3.2 S9.2.0 S10.1.1", "S7.2.1 S7.3.2 S10.1.2 W0",
+    "U0 S10.2.0 S11.1.2 S8.2.1", "S11.1.1 W1 S10.2.1 S7.3.0", "U1 S8.3.2 S9.2.1 f0.2", "S8.3.0 W2 S10.3.0 S11.2.1",
+    "U2 S9.3.0 S11.1.0 f1.2", "S5.3.1 f0.4 S6.3.1 S9.2.2", "f1.4 S7.3.1 S10.2.2 f0.1", "f2.2 f3.2 f0.6 S8.3.1",
+    "f2.4 f3.4 S9.3.2 S11.2.0", "S9.3.1 f1.6 S10.3.1 S11.3.1", "S11.2.2 S10.3.2 f1.1 f0.5", "f2.1 f2.6 f0.3 f3.1",
+    "S11.3.2 f3.6 S11.3.0 f2.3", "f1.3 f1.5 f3.3 f2.5", "f0.7 f3.5 f2.7 f1.7", "f3.7",
 ]
-PRODUCTS = [event[1:] for event in SCHEDULE if event[0] == "P"]
+EVENTS = [(e[0], [int(a) for a in e[1:].split(".") if a]) for group in SCHEDULE for e in group.split()]
+PRODUCTS = [tuple(args) for what, args in EVENTS if what == "P"]
 N_PROD = len(PRODUCTS)
 EARLY = 1
 FIRST_LATE = 4
@@ -78,7 +67,7 @@
 
 
 def kernel(x_hbm, dy_hbm, w_hbm, ainv_hbm, sinv_hbm, u_hbm, a_out, s_out,
-           act, wts, part, pair_buf, acc, stg, recv_g, recv_as, gsum, sinv, ainv, vfull, ustrip,
+           act, wts, part, pair_buf, acc, stg, recv_g, recv_as, recv_late, gsum, sinv, ainv, vfull, ustrip,
            load_sem, pair_send, pair_recv, credit, send_sem, recv_sem,
            v_send, v_recv, v_fwd_send, v_fwd_recv, v_pair_send, v_pair_recv,
            g_send, g_recv, gp_send, gp_recv, loc_sem):
@@ -122,7 +111,9 @@
             device_id_type=MESH,
         )
 
-    def landing(kind, j, u):
+    def landing(kind, j, u, step):
+        if kind != 2 and step > 0:
+            return recv_late.at[kind, j, u - 4]
         return recv_g.at[j, u] if kind == 2 else recv_as.at[kind, j, u]
 
     def staged(p, tx, j):
@@ -134,14 +125,14 @@
     def strip_copy(p, j, step, tx):
         kind, layer = PRODUCTS[p]
         u = unit(j, step, layer, tx)
-        if kind == 2:
+        if kind == 2 or step > 0:
             src = acc.at[p % SLOTS, tx, :, cols(j)]
         else:
             ref, idx = staged(p, tx, j)
             src = ref.at[idx]
         return pltpu.make_async_remote_copy(
             src_ref=src,
-            dst_ref=landing(kind, j, u),
+            dst_ref=landing(kind, j, u, step),
             send_sem=send_sem.at[p % SLOTS, j, tx],
             recv_sem=recv_sem.at[kind, j, u],
             device_id=(peer(ORDERS[j][step]),),
@@ -164,19 +155,29 @@
         for tx in range(2):
             pair_copy(p, tx).start()
 
+    def equal(dim, layer):
+        z_l, y_l = divmod(layer, 2)
+        return ybit == y_l if dim == 2 else zbit == z_l
+
     def drain(p):
         _, layer = PRODUCTS[p]
         for j in range(3):
-            strip_copy(p, j, 0, 1 - xbit).wait_send()
-
-        @pl.when(layer_own != layer)
-        def _():
-            for j in range(3):
-                strip_copy(p, j, 0, xbit).wait_send()
-
-    def equal(dim, layer):
-        z_l, y_l = divmod(layer, 2)
-        return ybit == y_l if dim == 2 else zbit == z_l
+            for step, dim in enumerate(ORDERS[j]):
+                before = ORDERS[j][:step]
+                sent_here = chip >= 0
+                for other in before:
+                    if other != 1:
+                        sent_here = jnp.logical_and(sent_here, equal(other, layer))
+                strips = [xbit] if 1 in before else [0, 1]
+                if dim == 1:
+                    strips = [1 - xbit]
+                else:
+                    sent_here = jnp.logical_and(sent_here, jnp.logical_not(equal(dim, layer)))
+
+                @pl.when(sent_here)
+                def _(j=j, step=step, strips=strips):
+                    for tx in strips:
+                        strip_copy(p, j, step, tx).wait_send()
 
     def stage(p, step, chunks=(0, 1, 2)):
         kind, layer = PRODUCTS[p]
@@ -196,13 +197,10 @@
                     for tx in strips:
                         strip_copy(p, j, step - 1, tx).wait_recv()
                         u = unit(j, step - 1, layer, tx)
-                        got = recv_g[j, u] if kind == 2 else recv_as[kind, j, u].astype(F32)
+                        got = landing(kind, j, u, step - 1)[...].astype(F32)
                         new = acc[slot, tx, :, cols(j)] + got
                         if step < 3:
                             acc[slot, tx, :, cols(j)] = new
-                        if kind != 2 and step < 3:
-                            ref, idx = staged(p, tx, j)
-                            ref[idx] = new.astype(BF16)
                 if step == 3:
                     if kind == 2:
                         gsum[:, cols(j)] = new * (1.0 / (ROWS * 16))
@@ -356,8 +354,7 @@
 
     loaded(0)
     n_prod = 0
-    for event in SCHEDULE:
-        what, args = event[0], event[1:]
+    for what, args in EVENTS:
         if what == "P":
             if args[0] == 1 or (args[0] == 2 and args[1] == 3):
                 loaded(2)
@@ -428,7 +425,8 @@
                 pltpu.VMEM((SLOTS, 2, STRIP, D), F32),
                 pltpu.VMEM((EARLY, 2, STRIP, D), BF16),
                 pltpu.VMEM((3, 7, STRIP, CHUNK), F32),
-                pltpu.VMEM((2, 3, 7, STRIP, CHUNK), BF16),
+                pltpu.VMEM((2, 3, 4, STRIP, CHUNK), BF16),
+                pltpu.VMEM((2, 3, 3, STRIP, CHUNK), F32),
                 pltpu.VMEM((STRIP, D), F32),
                 pltpu.VMEM((D, D), F32),
                 pltpu.VMEM((STRIP, D), F32),

time: 137 us -> 155 us (1.13)
  Pallas kernels: 137 us -> 153 us
    pallas_call x1, Pallas kernels: 129 us -> 146 us  [device_step(): pl.pallas_call(kernel, out_shape=(jax.ShapeDtypeStruct((N_LAYERS * D, D +...]
where the time goes in v3:
time: 155 us; the launch traced here: 154 us
  Pallas kernels  153 us (99%)
    pallas_call x1, Pallas kernels, device_step(): pl.pallas_call(kernel, out_shape=(jax.ShapeDtypeStruct((N_LAYERS * D, D +...  146 us
    pallas_call x1, Pallas kernels, device_step(): pl.pallas_call(tail, grid=(TAIL_STEPS,), out_shape=(jax.ShapeDtypeStruct(...  7.3 us

profile of v3, /device:TPU:0, one launch (start us, length us, event | category | flops | bytes accessed | tf_op | source)
XLA Modules:
  0.0 153.8 jit_solution(17192350858588835387)
XLA Ops:
  0.6 145.9 %shard_map.94 = (bf16[3072,896]{1,0:T(8,128)(2,1)}, f32[192,768]{1,0:T(8,128)}, f32[192,768]{1,0:T(8,128)}) custom-call(bf16[2048,768]{1,0:T(8,128)(2,1)} %x_hbm.1, bf16[2048,768]{1,0:T(8,128)(2,1)} %dy_hbm.1, bf16[4,768,768]{2,1,0:T(8,128)(2,1)} %w_hbm.1, f32[192,768]{1,0:T(8,128)} %ainv_hbm.1, f32[4,768,768]{2,1,0:T(8,128)} %sinv_hbm.1), custom_call_target="tpu_custom_call" | custom-call | tf_op jit(solution)/shard_map/pallas_call | solution.py:411
  146.5 7.3 %shard_map.95 = (f32[3072,768]{1,0:T(8,128)}, f32[192,768]{1,0:T(8,128)}, f32[192,768]{1,0:T(8,128)}) custom-call(bf16[3072,896]{1,0:T(8,128)(2,1)} %get-tuple-element.9.u_ref, f32[192,768]{1,0:T(8,128)} %a_old.1, f32[192,768]{1,0:T(8,128)} %get-tuple-element.10.a_sum, f32[192,768]{1,0:T(8,128)} %s_old.1, f32[192,768]{1,0:T(8,128)} %get-tuple-element.11.s_sum), custom_call_target="tpu_custom_call" | custom-call | tf_op jit(solution)/shard_map/pallas_call | solution.py:446

commit v4 on v3

--- a/solution.py
+++ b/solution.py
@@ -23,27 +23,27 @@
 GELU_K = 0.044715
 CONTRACT_ROWS = (((0,), (0,)), ((), ()))
 SCHEDULE = [
-    "F0 F1 F2 B3", "B2 P0.0 P2.2 R0", "P2.3 R1 P2.1 R2", "S0.1.0 S0.1.1 S0.1.2 B1", "R3 S1.1.0 P2.0 S1.1.1",
-    "S1.1.2 S2.1.0 S0.2.1 P1.2", "R4 S2.1.1 S0.2.0 S0.2.2", "P1.3 R5 S1.2.0 S1.2.2", "S2.1.2 S3.1.0 S3.1.2 S0.3.1",
-    "P0.2 R6 S3.1.1 P0.1", "S4.1.0 S4.1.1 S5.1.0 S2.2.0", "S2.2.1 S1.2.1 S4.1.2 S0.3.2", "S3.2.2 S0.3.0 R7 P1.1",
-    "S2.2.2 S3.2.0 S5.1.1 S5.1.2", "S6.1.0 S1.3.2 S1.3.0 S1.3.1", "R8 P1.0 S4.2.0 S4.2.2",
-    "S6.1.1 S6.1.2 S2.3.1 S3.2.1", "S4.2.1 S5.2.0 S7.1.0 S2.3.2", "S2.3.0 R9 S5.2.2 P0.3",
-    "S3.3.2 S3.3.0 S8.1.0 S7.1.2", "S6.2.2 S7.1.1 S6.2.0 S4.3.1", "S3.3.1 R10 S8.1.2 S8.1.1",
-    "S9.1.0 S4.3.0 S4.3.2 V", "R11 S5.2.1 S6.2.1 S7.2.0", "S7.2.2 S5.3.2 S5.3.0 S6.3.0",
-    "S10.1.0 S9.1.2 S8.2.2 S9.1.1", "S8.2.0 S6.3.2 S9.2.0 S10.1.1", "S7.2.1 S7.3.2 S10.1.2 W0",
-    "U0 S10.2.0 S11.1.2 S8.2.1", "S11.1.1 W1 S10.2.1 S7.3.0", "U1 S8.3.2 S9.2.1 f0.2", "S8.3.0 W2 S10.3.0 S11.2.1",
-    "U2 S9.3.0 S11.1.0 f1.2", "S5.3.1 f0.4 S6.3.1 S9.2.2", "f1.4 S7.3.1 S10.2.2 f0.1", "f2.2 f3.2 f0.6 S8.3.1",
-    "f2.4 f3.4 S9.3.2 S11.2.0", "S9.3.1 f1.6 S10.3.1 S11.3.1", "S11.2.2 S10.3.2 f1.1 f0.5", "f2.1 f2.6 f0.3 f3.1",
-    "S11.3.2 f3.6 S11.3.0 f2.3", "f1.3 f1.5 f3.3 f2.5", "f0.7 f3.5 f2.7 f1.7", "f3.7",
+    "F0 F1 P0.0 P0.1", "R0 F2 R1 P2.3", "S0.1.0 S0.1.1 S0.1.2 B3", "R2 S1.1.0 S1.1.1 S1.1.2",
+    "P2.2 S0.2.0 S0.2.2 B2", "R3 S2.1.0 S0.2.1 P2.1", "S2.1.1 S2.1.2 S0.3.0 S0.3.2", "S1.2.1 S1.2.2 B1 R4",
+    "S3.1.0 S1.2.0 P2.0 S2.2.0", "S2.2.2 S3.1.1 S3.1.2 S0.3.1", "S1.3.1 P1.2 R5 S3.2.0", "S4.1.0 S1.3.2 P0.3 R6",
+    "S2.2.1 S3.2.2 S4.1.2 P1.3", "R7 S3.2.1 S4.1.1 S1.3.0", "P1.1 R8 S2.3.0 S2.3.2", "S5.1.0 S5.1.1 S6.1.0 P1.0",
+    "S2.3.1 R9 S3.3.0 S4.2.0", "S4.2.2 S6.1.1 P0.2 S3.3.1", "S5.1.2 S6.1.2 S7.1.0 S7.1.1",
+    "S8.1.0 S3.3.2 R10 S7.1.2", "S8.1.1 S9.1.0 S5.2.1 S5.2.0", "S8.1.2 S6.2.0 S6.2.2 S9.1.1",
+    "S4.2.1 S5.2.2 S10.1.0 S4.3.2", "S9.1.2 S4.3.1 S4.3.0 R11", "S7.2.0 S7.2.1 S7.2.2 S10.1.1",
+    "S6.2.1 S5.3.1 S5.3.2 S5.3.0", "V S9.2.2 S8.2.0 S10.1.2", "S6.3.2 S6.3.0 S8.2.2 S11.1.0",
+    "S8.2.1 S10.2.0 S6.3.1 S11.1.1", "S10.2.1 S9.2.0 S7.3.2 S7.3.1", "S11.1.2 S8.3.2 S7.3.0 W0",
+    "U0 S11.2.0 S9.3.2 S9.2.1", "W1 S8.3.0 S11.2.1 S10.3.0", "U1 f0.2 S9.3.0 W2", "U2 f0.4 f1.2 S11.3.0",
+    "S8.3.1 S10.2.2 f1.4 S10.3.1", "f0.6 f2.4 S9.3.1 f3.4", "S11.3.1 S10.3.2 f2.2 f3.2", "S11.2.2 f0.1 f1.1 f1.6",
+    "f3.6 f2.1 S11.3.2 f3.1", "f0.3 f2.6 f2.5 f3.5", "f1.3 f3.3 f0.5 f2.3", "f3.7 f1.5 f2.7 f0.7", "f1.7",
 ]
 EVENTS = [(e[0], [int(a) for a in e[1:].split(".") if a]) for group in SCHEDULE for e in group.split()]
 PRODUCTS = [tuple(args) for what, args in EVENTS if what == "P"]
 N_PROD = len(PRODUCTS)
-EARLY = 1
-FIRST_LATE = 4
+EARLY = 2
+FIRST_LATE = 5
 ORDERS = [(1, 2, 4), (2, 4, 1), (4, 1, 2)]
 WIDE = 128
-PIECES = [(0, 256, (1, 2, 4)), (256, 256, (1, 4, 2)), (512, 256, (2, 4, 1)), (768, 128, (1, 2, 4))]
+PIECES = [(0, 256, (1, 2, 4)), (256, 256, (1, 2, 4)), (512, 256, (2, 4, 1)), (768, 128, (4, 1, 2))]
 
 
 def xor_chip(chip, mask):

time: 155 us -> 147 us (0.948)
  Pallas kernels: 153 us -> 146 us
    pallas_call x1, Pallas kernels: 146 us -> 139 us  [device_step(): pl.pallas_call(kernel, out_shape=(jax.ShapeDtypeStruct((N_LAYERS * D, D +...]
where the time goes in v4:
time: 147 us
  Pallas kernels  146 us (99%)
    pallas_call x1, Pallas kernels, device_step(): pl.pallas_call(kernel, out_shape=(jax.ShapeDtypeStruct((N_LAYERS * D, D +...  139 us
    pallas_call x1, Pallas kernels, device_step(): pl.pallas_call(tail, grid=(TAIL_STEPS,), out_shape=(jax.ShapeDtypeStruct(...  7.3 us

profile of v4, /device:TPU:0, one launch (start us, length us, event | category | flops | bytes accessed | tf_op | source)
XLA Modules:
  0.0 146.7 jit_solution(13918215074050388268)
XLA Ops:
  0.6 138.8 %shard_map.94 = (bf16[3072,896]{1,0:T(8,128)(2,1)}, f32[192,768]{1,0:T(8,128)}, f32[192,768]{1,0:T(8,128)}) custom-call(bf16[2048,768]{1,0:T(8,128)(2,1)} %x_hbm.1, bf16[2048,768]{1,0:T(8,128)(2,1)} %dy_hbm.1, bf16[4,768,768]{2,1,0:T(8,128)(2,1)} %w_hbm.1, f32[192,768]{1,0:T(8,128)} %ainv_hbm.1, f32[4,768,768]{2,1,0:T(8,128)} %sinv_hbm.1), custom_call_target="tpu_custom_call" | custom-call | tf_op jit(solution)/shard_map/pallas_call | solution.py:411
  139.4 7.3 %shard_map.95 = (f32[3072,768]{1,0:T(8,128)}, f32[192,768]{1,0:T(8,128)}, f32[192,768]{1,0:T(8,128)}) custom-call(bf16[3072,896]{1,0:T(8,128)(2,1)} %get-tuple-element.9.u_ref, f32[192,768]{1,0:T(8,128)} %a_old.1, f32[192,768]{1,0:T(8,128)} %get-tuple-element.10.a_sum, f32[192,768]{1,0:T(8,128)} %s_old.1, f32[192,768]{1,0:T(8,128)} %get-tuple-element.11.s_sum), custom_call_target="tpu_custom_call" | custom-call | tf_op jit(solution)/shard_map/pallas_call | solution.py:446
